TPU v7x, 32 devices: a whole 2x2x4 slice. The times are simulated.
32 devices in a mesh: chain: 4 (over z), inner: 8 (over y, x, core).
Axes of the slice: x: 2, y: 2, z: 4, core: 2. Of those that a mesh axis runs over, the one named last changes fastest.
Arguments:
- queries: bfloat16 [4096, 4096], P(('chain', 'inner')), may hold values from -0.75 to 0.75
- key_rows: bfloat16 [4096, 4096], P(('chain', 'inner')), may hold values from -0.75 to 0.75
- value_rows: bfloat16 [4096, 4096], P(('chain', 'inner')), may hold values from -0.75 to 0.75
- out_grad: bfloat16 [4096, 4096], P(('chain', 'inner')), may hold values from -0.75 to 0.75
- log_decay: bfloat16 [4096, 32], P(('chain', 'inner')), may hold values from -2 to 0, as said below
Outputs:
- attended: bfloat16 [4096, 4096], P(('chain', 'inner'))
- query_grad: bfloat16 [4096, 4096], P(('chain', 'inner'))
- key_grad: bfloat16 [4096, 4096], P(('chain', 'inner'))
- value_grad: bfloat16 [4096, 4096], P(('chain', 'inner'))
Inputs may be any that keep to these rules, and one draw needn't show every extreme that they name: `log_decay`: every entry is negative.
All inputs are finite; a program needn't handle non-finite values.
Results may differ from a plain program's by a relative error of at most 0.0051.
Values may be sent and summed in bfloat16 or wider, within the bound.
A program may use at most 64 MiB of HBM per device.

v0:
```python
import functools

import jax
import jax.numpy as jnp
from jax import lax
from jax.experimental import pallas as pl
from jax.experimental.pallas import tpu as pltpu
from jax.sharding import PartitionSpec as P

SIZE = 128
F32 = jnp.float32
BF16 = jnp.bfloat16
MESH = pl.DeviceIdType.MESH


def triangle(rows):
    row = lax.broadcasted_iota(jnp.int32, (rows, rows), 0)
    column = lax.broadcasted_iota(jnp.int32, (rows, rows), 1)
    return row >= column


def spread_column(decay, head):
    rows, heads = decay.shape
    pick = (lax.broadcasted_iota(jnp.int32, (heads, SIZE), 0) == head).astype(F32).astype(BF16)
    column = jnp.dot(decay, pick, preferred_element_type=F32).astype(BF16)
    lower = triangle(rows).astype(F32).astype(BF16)
    return jnp.dot(lower, column, preferred_element_type=F32), column


def over_rows(left, right):
    return lax.dot_general(left, right, (((0,), (0,)), ((), ())), preferred_element_type=F32)


def over_columns(left, right):
    return lax.dot_general(left, right, (((1,), (1,)), ((), ())), preferred_element_type=F32)


def states_kernel(
    planes, devices, q_ref, k_ref, v_ref, g_ref, decay_ref, states_ref,
    terms, from_core, to_chips, from_chips, plane_sum, from_planes, to_back, from_back, to_core,
    own_fin, core_fin, chip_fin, plane_fin,
    fin_s, fin_r, chip_fs, chip_fr, plane_fs, plane_fr,
    core_s, core_r, out_s, out_r, plane_s, plane_r, back_s, back_r, last_s, last_r,
):
    rows, heads = decay_ref.shape
    chips = devices // 2
    own = heads // devices
    z = lax.axis_index("chain")
    me = lax.axis_index("inner")
    chip, core = me // 2, lax.rem(me, 2)
    first_core = core == 0

    def at_core():
        return (z, chip * 2 + 1 - core)

    def at_chip(other):
        return (z, other * 2 + core)

    def at_plane(other):
        return (other, me)

    def remote(src, dst, send, recv, to):
        return pltpu.make_async_remote_copy(
            src_ref=src, dst_ref=dst, send_sem=send, recv_sem=recv, device_id=to, device_id_type=MESH
        )

    barrier = pltpu.get_barrier_semaphore()
    pl.semaphore_signal(barrier, inc=1, device_id=at_core(), device_id_type=MESH)
    for step in range(1, chips):
        pl.semaphore_signal(
            barrier, inc=1, device_id=at_chip(lax.rem(chip + step, chips)), device_id_type=MESH
        )
    for step in range(1, planes):
        pl.semaphore_signal(
            barrier, inc=1, device_id=at_plane(lax.rem(z + step, planes)), device_id_type=MESH
        )

    decay = decay_ref[...]
    own_fin[...] = over_rows(decay, jnp.ones((rows, SIZE), BF16))
    from_planes[z] = jnp.zeros(from_planes.shape[1:], BF16)
    pl.semaphore_wait(barrier, chips + planes - 1)

    fin_copy = remote(own_fin, core_fin, fin_s, fin_r, at_core())
    fin_copy.start()

    def make_terms(head):
        cumul, _ = spread_column(decay, head)
        columns = pl.ds(pl.multiple_of(head * SIZE, SIZE), SIZE)
        final = cumul[rows - 1 :, :]
        keys = (k_ref[:, columns].astype(F32) * jnp.exp(final - cumul)).astype(BF16)
        queries = (q_ref[:, columns].astype(F32) * jnp.exp(cumul)).astype(BF16)
        terms[head, 0] = over_rows(keys, v_ref[:, columns]).astype(BF16)
        terms[head, 1] = over_rows(queries, g_ref[:, columns]).astype(BF16)

    def core_copy(i, other):
        slot = other * own + i
        head = (other * 2 + 1 - core) * own + i
        return remote(
            terms.at[head], from_core.at[slot], core_s.at[slot], core_r.at[slot], at_core()
        )

    def first(i):
        @pl.loop(0, chips)
        def _(step):
            other = lax.rem(chip + 1 + step, chips)
            make_terms((other * 2 + 1 - core) * own + i)
            core_copy(i, other).start()

    def out_copy(i, other):
        return remote(
            to_chips.at[other, i], from_chips.at[chip, i], out_s.at[other * own + i],
            out_r.at[chip * own + i], at_chip(other),
        )

    def out_arrival(i, other):
        return remote(
            to_chips.at[other, i], from_chips.at[other, i], out_s.at[other * own + i],
            out_r.at[other * own + i], at_chip(other),
        )

    def second(i):
        @pl.loop(0, chips)
        def _(step):
            other = lax.rem(chip + 1 + step, chips)
            head = (other * 2 + core) * own + i
            make_terms(head)
            core_copy(i, other).wait_recv()
            slot = other * own + i
            mine = jnp.exp(own_fin[pl.ds(head, 1), :])
            theirs = jnp.exp(core_fin[pl.ds(head, 1), :])
            one = jnp.ones_like(mine)
            kv = (
                jnp.where(first_core, theirs, one) * terms[head, 0].astype(F32)
                + jnp.where(first_core, one, mine) * from_core[slot, 0].astype(F32)
            ).astype(BF16)
            qd = (
                jnp.where(first_core, one, theirs) * terms[head, 1].astype(F32)
                + jnp.where(first_core, mine, one) * from_core[slot, 1].astype(F32)
            ).astype(BF16)

            @pl.when(step < chips - 1)
            def _():
                to_chips[other, i, 0] = kv
                to_chips[other, i, 1] = qd
                out_copy(i, other).start()

            @pl.when(step == chips - 1)
            def _():
                from_chips[chip, i, 0] = kv
                from_chips[chip, i, 1] = qd

    first(0)
    fin_copy.wait_recv()
    chip_fin[chip] = own_fin[...] + core_fin[...]

    def chip_fin_copy(other, slot):
        return remote(
            chip_fin.at[chip], chip_fin.at[slot], chip_fs.at[other], chip_fr.at[slot], at_chip(other)
        )

    for step in range(1, chips):
        chip_fin_copy(lax.rem(chip + step, chips), chip).start()

    @pl.loop(0, own - 1)
    def _(i):
        second(i)
        first(i + 1)

    second(own - 1)

    for step in range(1, chips):
        other = lax.rem(chip + step, chips)
        chip_fin_copy(other, other).wait_recv()
    total = chip_fin[0]
    for other in range(1, chips):
        total = total + chip_fin[other]
    plane_fin[z] = total

    def plane_fin_copy(other, slot):
        return remote(
            plane_fin.at[z], plane_fin.at[slot], plane_fs.at[other], plane_fr.at[slot],
            at_plane(other),
        )

    for step in range(1, planes):
        plane_fin_copy(lax.rem(z + step, planes), z).start()

    def plane_copy(i, other, slot):
        kind = jnp.where(other > z, 0, 1)
        return remote(
            plane_sum.at[i, kind], from_planes.at[slot, i], plane_s.at[other * own + i],
            plane_r.at[slot * own + i], at_plane(other),
        )

    def sum_plane(i):
        head = me * own + i
        for step in range(1, chips):
            out_arrival(i, lax.rem(chip + step, chips)).wait_recv()
        kv = from_chips[0, i, 0].astype(F32)
        qd = from_chips[chips - 1, i, 1].astype(F32)
        for other in range(1, chips):
            kv = kv * jnp.exp(chip_fin[other, pl.ds(head, 1), :]) + from_chips[other, i, 0].astype(F32)
            back = chips - 1 - other
            qd = qd * jnp.exp(chip_fin[back, pl.ds(head, 1), :]) + from_chips[back, i, 1].astype(F32)
        plane_sum[i, 0] = kv.astype(BF16)
        plane_sum[i, 1] = qd.astype(BF16)
        for step in range(1, planes):
            plane_copy(i, lax.rem(z + step, planes), z).start()

    def back_copy(i, other):
        return remote(
            to_back.at[other, i], from_back.at[chip, i], back_s.at[other * own + i],
            back_r.at[chip * own + i], at_chip(other),
        )

    def back_arrival(i, other):
        return remote(
            to_back.at[other, i], from_back.at[other, i], back_s.at[other * own + i],
            back_r.at[other * own + i], at_chip(other),
        )

    def carry(i):
        head = me * own + i
        for step in range(1, planes):
            other = lax.rem(z + step, planes)
            plane_copy(i, other, other).wait_recv()
        kv = jnp.zeros((SIZE, SIZE), F32)
        qd = jnp.zeros((SIZE, SIZE), F32)
        for other in range(planes):
            factor = jnp.exp(plane_fin[other, pl.ds(head, 1), :])
            kv = jnp.where(other < z, kv * factor + from_planes[other, i].astype(F32), kv)
            back = planes - 1 - other
            factor = jnp.exp(plane_fin[back, pl.ds(head, 1), :])
            qd = jnp.where(back > z, qd * factor + from_planes[back, i].astype(F32), qd)
        for other in range(chips):
            to_back[other, i, 0] = kv.astype(BF16)
            back = chips - 1 - other
            to_back[back, i, 1] = qd.astype(BF16)
            if other < chips - 1:
                factor = jnp.exp(chip_fin[other, pl.ds(head, 1), :])
                kv = kv * factor + from_chips[other, i, 0].astype(F32)
                factor = jnp.exp(chip_fin[back, pl.ds(head, 1), :])
                qd = qd * factor + from_chips[back, i, 1].astype(F32)
        for step in range(1, chips):
            back_copy(i, lax.rem(chip + step, chips)).start()
        from_back[chip, i] = to_back[chip, i]

    def last_copy(i, other, side):
        head = (other * 2 + side) * own + i
        slot = other * own + i
        return remote(
            to_core.at[slot], states_ref.at[head], last_s.at[slot], last_r.at[slot], at_core()
        )

    def finish(i):
        @pl.loop(0, chips)
        def _(step):
            other = lax.rem(chip + step, chips)

            @pl.when(step > 0)
            def _():
                back_arrival(i, other).wait_recv()

            head = (other * 2 + core) * own + i
            slot = other * own + i
            mine = jnp.exp(own_fin[pl.ds(head, 1), :])
            theirs = jnp.exp(core_fin[pl.ds(head, 1), :])
            one = jnp.ones_like(mine)
            enter = from_back[other, i, 0].astype(F32)
            trail = from_back[other, i, 1].astype(F32)
            late = jnp.where(
                first_core, mine * enter + terms[head, 0].astype(F32),
                theirs * enter + from_core[slot, 0].astype(F32),
            )
            early = jnp.where(
                first_core, theirs * trail + from_core[slot, 1].astype(F32),
                mine * trail + terms[head, 1].astype(F32),
            )
            to_core[slot, 0] = jnp.where(first_core, late, enter).astype(BF16)
            to_core[slot, 1] = jnp.where(first_core, trail, early).astype(BF16)
            last_copy(i, other, core).start()
            states_ref[head, 0] = jnp.where(first_core, enter, late).astype(BF16)
            states_ref[head, 1] = jnp.where(first_core, early, trail).astype(BF16)

    lead = min(3, own)
    pl.loop(0, lead)(sum_plane)
    for step in range(1, planes):
        other = lax.rem(z + step, planes)
        plane_fin_copy(other, other).wait_recv()

    @pl.loop(0, own - lead)
    def _(i):
        carry(i)
        sum_plane(i + lead)

    pl.loop(own - lead, own)(carry)
    pl.loop(0, own)(finish)

    fin_copy.wait_send()
    for step in range(1, chips):
        chip_fin_copy(lax.rem(chip + step, chips), chip).wait_send()
    for step in range(1, planes):
        plane_fin_copy(lax.rem(z + step, planes), z).wait_send()

    @pl.loop(0, own)
    def _(i):
        @pl.loop(0, chips)
        def _(other):
            core_copy(i, other).wait_send()
            last_copy(i, other, core).wait_send()
            last_copy(i, other, 1 - core).wait_recv()

        @pl.loop(1, chips)
        def _(step):
            other = lax.rem(chip + step, chips)
            out_copy(i, other).wait_send()
            back_copy(i, other).wait_send()

        @pl.loop(1, planes)
        def _(step):
            plane_copy(i, lax.rem(z + step, planes), z).wait_send()


def carried_states(planes, devices, arrays):
    decay = arrays[-1]
    heads = decay.shape[1]
    chips, own = devices // 2, heads // devices
    square = (SIZE, SIZE)
    dma = pltpu.SemaphoreType.DMA
    slots = chips * own
    return pl.pallas_call(
        functools.partial(states_kernel, planes, devices),
        out_shape=jax.ShapeDtypeStruct((heads, 2) + square, BF16),
        in_specs=[pl.BlockSpec(memory_space=pltpu.VMEM)] * 5,
        out_specs=pl.BlockSpec(memory_space=pltpu.VMEM),
        scratch_shapes=[
            pltpu.VMEM((heads, 2) + square, BF16),
            pltpu.VMEM((slots, 2) + square, BF16),
            pltpu.VMEM((chips, own, 2) + square, BF16),
            pltpu.VMEM((chips, own, 2) + square, BF16),
            pltpu.VMEM((own, 2) + square, BF16),
            pltpu.VMEM((planes, own) + square, BF16),
            pltpu.VMEM((chips, own, 2) + square, BF16),
            pltpu.VMEM((chips, own, 2) + square, BF16),
            pltpu.VMEM((slots, 2) + square, BF16),
            pltpu.VMEM((heads, SIZE), F32),
            pltpu.VMEM((heads, SIZE), F32),
            pltpu.VMEM((chips, heads, SIZE), F32),
            pltpu.VMEM((planes, heads, SIZE), F32),
            dma, dma, dma((chips,)), dma((chips,)), dma((planes,)), dma((planes,)),
            dma((slots,)), dma((slots,)), dma((slots,)), dma((slots,)),
            dma((planes * own,)), dma((planes * own,)),
            dma((slots,)), dma((slots,)), dma((slots,)), dma((slots,)),
        ],
        compiler_params=pltpu.CompilerParams(
            collective_id=0, has_side_effects=True, vmem_limit_bytes=40 * 2**20
        ),
    )(*arrays)


def block_kernel(
    group, q_ref, k_ref, v_ref, g_ref, decay_ref, states_ref, o_ref, dq_ref, dk_ref, dv_ref
):
    decay = decay_ref[...]
    rows = decay.shape[0]
    lower = triangle(rows)
    for i in range(group):
        head = pl.program_id(0) * group + i
        columns = slice(i * SIZE, (i + 1) * SIZE)
        query, key, value, grad = (ref[:, columns] for ref in (q_ref, k_ref, v_ref, g_ref))
        enter, trail = states_ref[i, 0], states_ref[i, 1]
        cumul, column = spread_column(decay, head)
        upper = (
            lax.broadcasted_iota(jnp.int32, (rows, rows), 0)
            <= lax.broadcasted_iota(jnp.int32, (rows, rows), 1)
        ).astype(F32).astype(BF16)
        across = over_rows(column, upper)
        weights = jnp.exp(jnp.where(lower, cumul - across, -jnp.inf))
        forward = jnp.exp(cumul)
        backward = jnp.exp(cumul[rows - 1 :, :] - cumul)
        probs = (over_columns(query, key) * weights).astype(BF16)
        grows = (over_columns(grad, value) * weights).astype(BF16)
        o_ref[:, columns] = (
            jnp.dot(probs, value, preferred_element_type=F32)
            + forward * jnp.dot(query, enter, preferred_element_type=F32)
        ).astype(BF16)
        dq_ref[:, columns] = (
            jnp.dot(grows, key, preferred_element_type=F32) + forward * over_columns(grad, enter)
        ).astype(BF16)
        dk_ref[:, columns] = (
            over_rows(grows, query) + backward * over_columns(value, trail)
        ).astype(BF16)
        dv_ref[:, columns] = (
            over_rows(probs, grad) + backward * jnp.dot(key, trail, preferred_element_type=F32)
        ).astype(BF16)


def block_results(arrays, states):
    rows, heads = arrays[-1].shape
    group = 4
    wide = pl.BlockSpec((rows, group * SIZE), lambda i: (0, i))
    return pl.pallas_call(
        functools.partial(block_kernel, group),
        grid=(heads // group,),
        out_shape=[jax.ShapeDtypeStruct(arrays[0].shape, BF16)] * 4,
        in_specs=[wide] * 4
        + [
            pl.BlockSpec((rows, heads), lambda i: (0, 0)),
            pl.BlockSpec((group, 2, SIZE, SIZE), lambda i: (i, 0, 0, 0)),
        ],
        out_specs=[wide] * 4,
    )(*arrays, states)


def solution(mesh):
    planes, devices = mesh.shape["chain"], mesh.shape["inner"]

    def shards(*arrays):
        return tuple(block_results(arrays, carried_states(planes, devices, arrays)))

    spec = P(("chain", "inner"), None)
    return jax.shard_map(
        shards, mesh=mesh, in_specs=(spec,) * 5, out_specs=(spec,) * 4, check_vma=False
    )
```

profile of v0, /device:TPU:0, one launch (start us, length us, event | category | flops | bytes accessed | tf_op | source)
XLA Modules:
  0.0 68.6 jit_solution(7580407912439780814)
XLA Ops:
  0.6 0.8 %copy.10.decay_ref = bf16[128,32]{1,0:T(8,128)(2,1)S(1)} copy(bf16[128,32]{0,1:T(8,128)(2,1)} %param.9) | data formatting | bytes 16384 | tf_op args[4]
  1.4 0.0 copy-start.1
  1.4 1.2 %copy-done.1 = bf16[128,4096]{1,0:T(8,128)(2,1)S(1)} copy-done((bf16[128,4096]{1,0:T(8,128)(2,1)S(1)}, bf16[128,4096]{1,0:T(8,128)(2,1)}, u32[]{:S(2)}) %copy-start.1) | copy-done | bytes 1048600
  2.7 0.0 copy-start.2
  2.7 1.2 %copy-done.2 = bf16[128,4096]{1,0:T(8,128)(2,1)S(1)} copy-done((bf16[128,4096]{1,0:T(8,128)(2,1)S(1)}, bf16[128,4096]{1,0:T(8,128)(2,1)}, u32[]{:S(2)}) %copy-start.2) | copy-done | bytes 1048600
  3.9 0.0 copy-start.3
  3.9 1.2 %copy-done.3 = bf16[128,4096]{1,0:T(8,128)(2,1)S(1)} copy-done((bf16[128,4096]{1,0:T(8,128)(2,1)S(1)}, bf16[128,4096]{1,0:T(8,128)(2,1)}, u32[]{:S(2)}) %copy-start.3) | copy-done | bytes 1048600
  5.1 0.0 copy-start.4
  5.1 1.2 %copy-done.4 = bf16[128,4096]{1,0:T(8,128)(2,1)S(1)} copy-done((bf16[128,4096]{1,0:T(8,128)(2,1)S(1)}, bf16[128,4096]{1,0:T(8,128)(2,1)}, u32[]{:S(2)}) %copy-start.4) | copy-done | bytes 1048600
  6.3 0.0 copy-start.5
  6.4 43.8 %shard_map.84.states_ref = bf16[32,2,128,128]{3,2,1,0:T(8,128)(2,1)S(1)} custom-call(bf16[128,4096]{1,0:T(8,128)(2,1)S(1)} %copy-done.1, bf16[128,4096]{1,0:T(8,128)(2,1)S(1)} %copy-done.2, bf16[128,4096]{1,0:T(8,128)(2,1)S(1)} %copy-done.3, bf16[128,4096]{1,0:T(8,128)(2,1)S(1)} %copy-done.4, bf16[128,32]{1,0:T(8,128)(2,1)S(1)} %copy.10.decay_ref), custom_call_target="tpu_custom_call" | custom-call | tf_op jit(solution)/shard_map/pallas_call | solution.py:331
  50.1 0.0 copy-done.5
  50.1 0.0 copy-start
  50.2 1.3 %copy-done = bf16[32,2,128,128]{3,2,1,0:T(8,128)(2,1)} copy-done((bf16[32,2,128,128]{3,2,1,0:T(8,128)(2,1)}, bf16[32,2,128,128]{3,2,1,0:T(8,128)(2,1)S(1)}, u32[]{:S(2)}) %copy-start) | copy-done | bytes 2097176
  51.5 17.1 %shard_map.85 = (bf16[128,4096]{1,0:T(8,128)(2,1)}, bf16[128,4096]{1,0:T(8,128)(2,1)}, bf16[128,4096]{1,0:T(8,128)(2,1)}, bf16[128,4096]{1,0:T(8,128)(2,1)}) custom-call(bf16[128,4096]{1,0:T(8,128)(2,1)} %q_ref.3, bf16[128,4096]{1,0:T(8,128)(2,1)} %k_ref.3, bf16[128,4096]{1,0:T(8,128)(2,1)} %v_ref.3, bf16[128,4096]{1,0:T(8,128)(2,1)} %g_ref.3, ...), custom_call_target="tpu_custom_call" | custom-call | tf_op jit(solution)/shard_map/pallas_call | solution.py:402
Async XLA Ops:
  1.4 1.2 %copy-start.1 = (bf16[128,4096]{1,0:T(8,128)(2,1)S(1)}, bf16[128,4096]{1,0:T(8,128)(2,1)}, u32[]{:S(2)}) copy-start(bf16[128,4096]{1,0:T(8,128)(2,1)} %q_ref.3) | copy-start | bytes 3145732
  2.7 1.2 %copy-start.2 = (bf16[128,4096]{1,0:T(8,128)(2,1)S(1)}, bf16[128,4096]{1,0:T(8,128)(2,1)}, u32[]{:S(2)}) copy-start(bf16[128,4096]{1,0:T(8,128)(2,1)} %k_ref.3) | copy-start | bytes 3145732
  3.9 1.2 %copy-start.3 = (bf16[128,4096]{1,0:T(8,128)(2,1)S(1)}, bf16[128,4096]{1,0:T(8,128)(2,1)}, u32[]{:S(2)}) copy-start(bf16[128,4096]{1,0:T(8,128)(2,1)} %v_ref.3) | copy-start | bytes 3145732
  5.1 1.2 %copy-start.4 = (bf16[128,4096]{1,0:T(8,128)(2,1)S(1)}, bf16[128,4096]{1,0:T(8,128)(2,1)}, u32[]{:S(2)}) copy-start(bf16[128,4096]{1,0:T(8,128)(2,1)} %g_ref.3) | copy-start | bytes 3145732
  6.3 43.8 %copy-start.5 = (bf16[128,32]{1,0:T(8,128)(2,1)}, bf16[128,32]{1,0:T(8,128)(2,1)S(1)}, u32[]{:S(2)}) copy-start(bf16[128,32]{1,0:T(8,128)(2,1)S(1)} %copy.10.decay_ref) | copy-start | bytes 24580
  50.1 1.3 %copy-start = (bf16[32,2,128,128]{3,2,1,0:T(8,128)(2,1)}, bf16[32,2,128,128]{3,2,1,0:T(8,128)(2,1)S(1)}, u32[]{:S(2)}) copy-start(bf16[32,2,128,128]{3,2,1,0:T(8,128)(2,1)S(1)} %shard_map.84.states_ref) | copy-start | bytes 6291460
where the time goes:
time: 69 us; the launch traced here: 68.6 us
  Pallas kernels  60.9 us (88%)
  local copies, waits for them, and re-layouts  7.05 us (10%)
    pallas_call x1, Pallas kernels, carried_states(): pl.pallas_call(functools.partial(states_kernel, planes, devices), out_sha...  43.8 us
    pallas_call x1, Pallas kernels, block_results(): pl.pallas_call(functools.partial(block_kernel, group), grid=(heads // gro...  17.1 us
    unnamed x13, local copies, waits for them, and re-layouts  7.05 us

commit v1 on v0

--- a/solution.py
+++ b/solution.py
@@ -24,7 +24,7 @@
     pick = (lax.broadcasted_iota(jnp.int32, (heads, SIZE), 0) == head).astype(F32).astype(BF16)
     column = jnp.dot(decay, pick, preferred_element_type=F32).astype(BF16)
     lower = triangle(rows).astype(F32).astype(BF16)
-    return jnp.dot(lower, column, preferred_element_type=F32), column
+    return jnp.dot(lower, column, preferred_element_type=F32)
 
 
 def over_rows(left, right):
@@ -36,10 +36,11 @@
 
 
 def states_kernel(
-    planes, devices, q_ref, k_ref, v_ref, g_ref, decay_ref, states_ref,
-    terms, from_core, to_chips, from_chips, plane_sum, from_planes, to_back, from_back, to_core,
+    planes, devices, q_any, k_any, v_any, g_any, decay_ref, states_ref,
+    q_ref, k_ref, v_ref, g_ref, cumuls, local,
+    cumul_rows, terms, from_core, to_chips, from_chips, plane_sum, from_planes, to_back, from_back, to_core,
     own_fin, core_fin, chip_fin, plane_fin,
-    fin_s, fin_r, chip_fs, chip_fr, plane_fs, plane_fr,
+    load_s, fin_s, fin_r, chip_fs, chip_fr, plane_fs, plane_fr,
     core_s, core_r, out_s, out_r, plane_s, plane_r, back_s, back_r, last_s, last_r,
 ):
     rows, heads = decay_ref.shape
@@ -64,6 +65,31 @@
             src_ref=src, dst_ref=dst, send_sem=send, recv_sem=recv, device_id=to, device_id_type=MESH
         )
 
+    def loads(group, part):
+        begin, width = (0, SIZE) if part == 0 else (SIZE, (own - 1) * SIZE)
+        columns = pl.ds(pl.multiple_of(group * (own * SIZE) + begin, SIZE), width)
+        pairs = ((q_any, q_ref), (k_any, k_ref), (v_any, v_ref), (g_any, g_ref))
+        return [
+            pltpu.make_async_copy(src.at[:, columns], dst.at[:, columns], load_s.at[j, group, part])
+            for j, (src, dst) in enumerate(pairs)
+        ]
+
+    def owner(step, side):
+        return lax.rem(chip + 1 + step, chips) * 2 + side
+
+    for side in (1 - core, core):
+        @pl.loop(0, chips)
+        def _(step):
+            for copy in loads(owner(step, side), 0):
+                copy.start()
+
+    if own > 1:
+        for side in (1 - core, core):
+            @pl.loop(0, chips)
+            def _(step):
+                for copy in loads(owner(step, side), 1):
+                    copy.start()
+
     barrier = pltpu.get_barrier_semaphore()
     pl.semaphore_signal(barrier, inc=1, device_id=at_core(), device_id_type=MESH)
     for step in range(1, chips):
@@ -77,6 +103,11 @@
 
     decay = decay_ref[...]
     own_fin[...] = over_rows(decay, jnp.ones((rows, SIZE), BF16))
+    upper = jnp.logical_not(triangle(rows)) | (
+        lax.broadcasted_iota(jnp.int32, (rows, rows), 0)
+        == lax.broadcasted_iota(jnp.int32, (rows, rows), 1)
+    )
+    cumul_rows[...] = over_rows(decay, upper.astype(F32).astype(BF16))
     from_planes[z] = jnp.zeros(from_planes.shape[1:], BF16)
     pl.semaphore_wait(barrier, chips + planes - 1)
 
@@ -84,13 +115,34 @@
     fin_copy.start()
 
     def make_terms(head):
-        cumul, _ = spread_column(decay, head)
+        cumul = spread_column(decay, head)
+        cumuls[head] = cumul
         columns = pl.ds(pl.multiple_of(head * SIZE, SIZE), SIZE)
         final = cumul[rows - 1 :, :]
         keys = (k_ref[:, columns].astype(F32) * jnp.exp(final - cumul)).astype(BF16)
         queries = (q_ref[:, columns].astype(F32) * jnp.exp(cumul)).astype(BF16)
-        terms[head, 0] = over_rows(keys, v_ref[:, columns]).astype(BF16)
-        terms[head, 1] = over_rows(queries, g_ref[:, columns]).astype(BF16)
+        terms[head, 0] = over_rows(keys, v_ref[:, columns])
+        terms[head, 1] = over_rows(queries, g_ref[:, columns])
+
+    def inside(head):
+        columns = pl.ds(pl.multiple_of(head * SIZE, SIZE), SIZE)
+        query, key, value, grad = (ref[:, columns] for ref in (q_ref, k_ref, v_ref, g_ref))
+        spread = cumuls[head] - cumul_rows[pl.ds(head, 1), :]
+        weights = jnp.exp(jnp.where(triangle(rows), spread, -jnp.inf))
+        probs = (over_columns(query, key) * weights).astype(BF16)
+        grows = (over_columns(grad, value) * weights).astype(BF16)
+        local[0, head] = jnp.dot(probs, value, preferred_element_type=F32)
+        local[1, head] = jnp.dot(grows, key, preferred_element_type=F32)
+        local[2, head] = over_rows(grows, query)
+        local[3, head] = over_rows(probs, grad)
+
+    chunk = heads // 8
+
+    def inside_chunk(at):
+        @pl.loop(0, chunk // 2)
+        def _(pair):
+            for j in range(2):
+                inside(at * chunk + pair * 2 + j)
 
     def core_copy(i, other):
         slot = other * own + i
@@ -99,12 +151,21 @@
             terms.at[head], from_core.at[slot], core_s.at[slot], core_r.at[slot], at_core()
         )
 
-    def first(i):
-        @pl.loop(0, chips)
-        def _(step):
-            other = lax.rem(chip + 1 + step, chips)
-            make_terms((other * 2 + 1 - core) * own + i)
-            core_copy(i, other).start()
+    def wait_loads(step, side):
+        for copy in loads(owner(step, side), 0):
+            copy.wait()
+
+    def first(i, loading=False):
+        @pl.loop(0, chips // 2)
+        def _(pair):
+            steps = (pair * 2, pair * 2 + 1)
+            for step in steps:
+                if loading:
+                    wait_loads(step, 1 - core)
+            for step in steps:
+                make_terms(owner(step, 1 - core) * own + i)
+            for step in steps:
+                core_copy(i, lax.rem(chip + 1 + step, chips)).start()
 
     def out_copy(i, other):
         return remote(
@@ -118,24 +179,35 @@
             out_r.at[other * own + i], at_chip(other),
         )
 
-    def second(i):
-        @pl.loop(0, chips)
-        def _(step):
+    def second(i, loading=False):
+        @pl.loop(0, chips // 2)
+        def _(pair):
+            steps = (pair * 2, pair * 2 + 1)
+            for step in steps:
+                if loading:
+                    wait_loads(step, core)
+            for step in steps:
+                make_terms(owner(step, core) * own + i)
+            for step in steps:
+                core_copy(i, lax.rem(chip + 1 + step, chips)).wait_recv()
+            for step in steps:
+                combine(i, step)
+
+    def combine(i, step):
+        if True:
             other = lax.rem(chip + 1 + step, chips)
             head = (other * 2 + core) * own + i
-            make_terms(head)
-            core_copy(i, other).wait_recv()
             slot = other * own + i
             mine = jnp.exp(own_fin[pl.ds(head, 1), :])
             theirs = jnp.exp(core_fin[pl.ds(head, 1), :])
             one = jnp.ones_like(mine)
             kv = (
-                jnp.where(first_core, theirs, one) * terms[head, 0].astype(F32)
-                + jnp.where(first_core, one, mine) * from_core[slot, 0].astype(F32)
+                jnp.where(first_core, theirs, one) * terms[head, 0]
+                + jnp.where(first_core, one, mine) * from_core[slot, 0]
             ).astype(BF16)
             qd = (
-                jnp.where(first_core, one, theirs) * terms[head, 1].astype(F32)
-                + jnp.where(first_core, mine, one) * from_core[slot, 1].astype(F32)
+                jnp.where(first_core, one, theirs) * terms[head, 1]
+                + jnp.where(first_core, mine, one) * from_core[slot, 1]
             ).astype(BF16)
 
             @pl.when(step < chips - 1)
@@ -149,7 +221,7 @@
                 from_chips[chip, i, 0] = kv
                 from_chips[chip, i, 1] = qd
 
-    first(0)
+    first(0, True)
     fin_copy.wait_recv()
     chip_fin[chip] = own_fin[...] + core_fin[...]
 
@@ -161,12 +233,17 @@
     for step in range(1, chips):
         chip_fin_copy(lax.rem(chip + step, chips), chip).start()
 
-    @pl.loop(0, own - 1)
-    def _(i):
-        second(i)
-        first(i + 1)
-
-    second(own - 1)
+    second(0, True)
+    if own > 1:
+        @pl.loop(0, devices)
+        def _(group):
+            for copy in loads(group, 1):
+                copy.wait()
+
+        @pl.loop(1, own)
+        def _(i):
+            first(i)
+            second(i)
 
     for step in range(1, chips):
         other = lax.rem(chip + step, chips)
@@ -269,12 +346,12 @@
             enter = from_back[other, i, 0].astype(F32)
             trail = from_back[other, i, 1].astype(F32)
             late = jnp.where(
-                first_core, mine * enter + terms[head, 0].astype(F32),
-                theirs * enter + from_core[slot, 0].astype(F32),
+                first_core, mine * enter + terms[head, 0],
+                theirs * enter + from_core[slot, 0],
             )
             early = jnp.where(
-                first_core, theirs * trail + from_core[slot, 1].astype(F32),
-                mine * trail + terms[head, 1].astype(F32),
+                first_core, theirs * trail + from_core[slot, 1],
+                mine * trail + terms[head, 1],
             )
             to_core[slot, 0] = jnp.where(first_core, late, enter).astype(BF16)
             to_core[slot, 1] = jnp.where(first_core, trail, early).astype(BF16)
@@ -282,18 +359,27 @@
             states_ref[head, 0] = jnp.where(first_core, enter, late).astype(BF16)
             states_ref[head, 1] = jnp.where(first_core, early, trail).astype(BF16)
 
+    events = []
     lead = min(3, own)
-    pl.loop(0, lead)(sum_plane)
-    for step in range(1, planes):
-        other = lax.rem(z + step, planes)
-        plane_fin_copy(other, other).wait_recv()
-
-    @pl.loop(0, own - lead)
-    def _(i):
-        carry(i)
-        sum_plane(i + lead)
-
-    pl.loop(own - lead, own)(carry)
+    for i in range(lead):
+        events.append((sum_plane, i))
+    for i in range(own):
+        events.append((carry, i))
+        if i + lead < own:
+            events.append((sum_plane, i + lead))
+    done = 0
+    waited = False
+    for at, (event, i) in enumerate(events):
+        if event is carry and not waited:
+            waited = True
+            for step in range(1, planes):
+                other = lax.rem(z + step, planes)
+                plane_fin_copy(other, other).wait_recv()
+        event(i)
+        until = 8 * (at + 1) // len(events)
+        for part in range(done, until):
+            inside_chunk(part)
+        done = until
     pl.loop(0, own)(finish)
 
     fin_copy.wait_send()
@@ -330,12 +416,19 @@
     slots = chips * own
     return pl.pallas_call(
         functools.partial(states_kernel, planes, devices),
-        out_shape=jax.ShapeDtypeStruct((heads, 2) + square, BF16),
-        in_specs=[pl.BlockSpec(memory_space=pltpu.VMEM)] * 5,
-        out_specs=pl.BlockSpec(memory_space=pltpu.VMEM),
+        out_shape=[jax.ShapeDtypeStruct((heads, 2) + square, BF16)]
+        + [jax.ShapeDtypeStruct(arrays[0].shape, BF16)] * 4
+        + [
+            jax.ShapeDtypeStruct((heads,) + square, F32),
+            jax.ShapeDtypeStruct((4, heads) + square, F32),
+        ],
+        in_specs=[pl.BlockSpec(memory_space=pltpu.HBM)] * 4
+        + [pl.BlockSpec(memory_space=pltpu.VMEM)],
+        out_specs=[pl.BlockSpec(memory_space=pltpu.VMEM)] * 7,
         scratch_shapes=[
-            pltpu.VMEM((heads, 2) + square, BF16),
-            pltpu.VMEM((slots, 2) + square, BF16),
+            pltpu.VMEM((heads, SIZE), F32),
+            pltpu.VMEM((heads, 2) + square, F32),
+            pltpu.VMEM((slots, 2) + square, F32),
             pltpu.VMEM((chips, own, 2) + square, BF16),
             pltpu.VMEM((chips, own, 2) + square, BF16),
             pltpu.VMEM((own, 2) + square, BF16),
@@ -347,76 +440,57 @@
             pltpu.VMEM((heads, SIZE), F32),
             pltpu.VMEM((chips, heads, SIZE), F32),
             pltpu.VMEM((planes, heads, SIZE), F32),
-            dma, dma, dma((chips,)), dma((chips,)), dma((planes,)), dma((planes,)),
+            dma((4, devices, 2)), dma, dma, dma((chips,)), dma((chips,)), dma((planes,)), dma((planes,)),
             dma((slots,)), dma((slots,)), dma((slots,)), dma((slots,)),
             dma((planes * own,)), dma((planes * own,)),
             dma((slots,)), dma((slots,)), dma((slots,)), dma((slots,)),
         ],
         compiler_params=pltpu.CompilerParams(
-            collective_id=0, has_side_effects=True, vmem_limit_bytes=40 * 2**20
+            collective_id=0, has_side_effects=True, vmem_limit_bytes=20 * 2**20
         ),
     )(*arrays)
 
 
 def block_kernel(
-    group, q_ref, k_ref, v_ref, g_ref, decay_ref, states_ref, o_ref, dq_ref, dk_ref, dv_ref
+    group, states_ref, q_ref, k_ref, v_ref, g_ref, cumuls, local, o_ref, dq_ref, dk_ref, dv_ref
 ):
-    decay = decay_ref[...]
-    rows = decay.shape[0]
-    lower = triangle(rows)
     for i in range(group):
         head = pl.program_id(0) * group + i
         columns = slice(i * SIZE, (i + 1) * SIZE)
-        query, key, value, grad = (ref[:, columns] for ref in (q_ref, k_ref, v_ref, g_ref))
-        enter, trail = states_ref[i, 0], states_ref[i, 1]
-        cumul, column = spread_column(decay, head)
-        upper = (
-            lax.broadcasted_iota(jnp.int32, (rows, rows), 0)
-            <= lax.broadcasted_iota(jnp.int32, (rows, rows), 1)
-        ).astype(F32).astype(BF16)
-        across = over_rows(column, upper)
-        weights = jnp.exp(jnp.where(lower, cumul - across, -jnp.inf))
+        taken = pl.ds(pl.multiple_of(head * SIZE, SIZE), SIZE)
+        query, key, value, grad = (ref[:, taken] for ref in (q_ref, k_ref, v_ref, g_ref))
+        enter, trail = states_ref[head, 0], states_ref[head, 1]
+        cumul = cumuls[head]
         forward = jnp.exp(cumul)
-        backward = jnp.exp(cumul[rows - 1 :, :] - cumul)
-        probs = (over_columns(query, key) * weights).astype(BF16)
-        grows = (over_columns(grad, value) * weights).astype(BF16)
+        backward = jnp.exp(cumul[-1:, :] - cumul)
         o_ref[:, columns] = (
-            jnp.dot(probs, value, preferred_element_type=F32)
-            + forward * jnp.dot(query, enter, preferred_element_type=F32)
+            local[0, head] + forward * jnp.dot(query, enter, preferred_element_type=F32)
         ).astype(BF16)
-        dq_ref[:, columns] = (
-            jnp.dot(grows, key, preferred_element_type=F32) + forward * over_columns(grad, enter)
+        dq_ref[:, columns] = (local[1, head] + forward * over_columns(grad, enter)).astype(BF16)
+        dk_ref[:, columns] = (local[2, head] + backward * over_columns(value, trail)).astype(BF16)
+        dv_ref[:, columns] = (
+            local[3, head] + backward * jnp.dot(key, trail, preferred_element_type=F32)
         ).astype(BF16)
-        dk_ref[:, columns] = (
-            over_rows(grows, query) + backward * over_columns(value, trail)
-        ).astype(BF16)
-        dv_ref[:, columns] = (
-            over_rows(probs, grad) + backward * jnp.dot(key, trail, preferred_element_type=F32)
-        ).astype(BF16)
-
-
-def block_results(arrays, states):
-    rows, heads = arrays[-1].shape
+
+
+def block_results(held):
+    rows, features = held[1].shape
     group = 4
-    wide = pl.BlockSpec((rows, group * SIZE), lambda i: (0, i))
     return pl.pallas_call(
         functools.partial(block_kernel, group),
-        grid=(heads // group,),
-        out_shape=[jax.ShapeDtypeStruct(arrays[0].shape, BF16)] * 4,
-        in_specs=[wide] * 4
-        + [
-            pl.BlockSpec((rows, heads), lambda i: (0, 0)),
-            pl.BlockSpec((group, 2, SIZE, SIZE), lambda i: (i, 0, 0, 0)),
-        ],
-        out_specs=[wide] * 4,
-    )(*arrays, states)
+        grid=(features // (group * SIZE),),
+        out_shape=[jax.ShapeDtypeStruct((rows, features), BF16)] * 4,
+        in_specs=[pl.BlockSpec(memory_space=pltpu.VMEM)] * 7,
+        out_specs=[pl.BlockSpec((rows, group * SIZE), lambda i: (0, i))] * 4,
+        compiler_params=pltpu.CompilerParams(vmem_limit_bytes=8 * 2**20),
+    )(*held)
 
 
 def solution(mesh):
     planes, devices = mesh.shape["chain"], mesh.shape["inner"]
 
     def shards(*arrays):
-        return tuple(block_results(arrays, carried_states(planes, devices, arrays)))
+        return tuple(block_results(carried_states(planes, devices, arrays)))
 
     spec = P(("chain", "inner"), None)
     return jax.shard_map(

time: 69 us -> 55.3 us (0.80)
  Pallas kernels: 60.9 us -> 48.6 us
  local copies, waits for them, and re-layouts: 7.05 us -> 5.71 us
    pallas_call x1, Pallas kernels: 17.1 us -> 4.89 us  [block_results(): pl.pallas_call(functools.partial(block_kernel, group), grid=(features //...]
    unnamed x13 -> x9, local copies, waits for them, and re-layouts: 7.05 us -> 5.71 us
where the time goes in v1:
time: 55.3 us; the launch traced here: 55 us
  Pallas kernels  48.6 us (88%)
  local copies, waits for them, and re-layouts  5.71 us (10%)
  between operations  0.65 us (1%)
    pallas_call x1, Pallas kernels, carried_states(): pl.pallas_call(functools.partial(states_kernel, planes, devices), out_sha...  43.7 us
    unnamed x9, local copies, waits for them, and re-layouts  5.71 us
    pallas_call x1, Pallas kernels, block_results(): pl.pallas_call(functools.partial(block_kernel, group), grid=(features //...  4.89 us

profile of v1, /device:TPU:0, one launch (start us, length us, event | category | flops | bytes accessed | tf_op | source)
XLA Modules:
  0.0 55.0 jit_solution(13494348570076164450)
XLA Ops:
  0.6 0.8 %copy.9.decay_ref = bf16[128,32]{1,0:T(8,128)(2,1)S(1)} copy(bf16[128,32]{0,1:T(8,128)(2,1)} %param.9) | data formatting | bytes 16384 | tf_op args[4]
  1.4 0.0 copy-start
  1.4 1.2 %copy-done = bf16[128,4096]{1,0:T(8,128)(2,1)S(1)} copy-done((bf16[128,4096]{1,0:T(8,128)(2,1)S(1)}, bf16[128,4096]{1,0:T(8,128)(2,1)}, u32[]{:S(2)}) %copy-start) | copy-done | bytes 1048600
  2.7 0.0 copy-start.1
  2.7 1.2 %copy-done.1 = bf16[128,4096]{1,0:T(8,128)(2,1)S(1)} copy-done((bf16[128,4096]{1,0:T(8,128)(2,1)S(1)}, bf16[128,4096]{1,0:T(8,128)(2,1)}, u32[]{:S(2)}) %copy-start.1) | copy-done | bytes 1048600
  3.9 0.0 copy-start.2
  3.9 1.2 %copy-done.2 = bf16[128,4096]{1,0:T(8,128)(2,1)S(1)} copy-done((bf16[128,4096]{1,0:T(8,128)(2,1)S(1)}, bf16[128,4096]{1,0:T(8,128)(2,1)}, u32[]{:S(2)}) %copy-start.2) | copy-done | bytes 1048600
  5.1 0.0 copy-start.3
  5.1 1.2 %copy-done.3 = bf16[128,4096]{1,0:T(8,128)(2,1)S(1)} copy-done((bf16[128,4096]{1,0:T(8,128)(2,1)S(1)}, bf16[128,4096]{1,0:T(8,128)(2,1)}, u32[]{:S(2)}) %copy-start.3) | copy-done | bytes 1048600
  6.3 43.7 %shard_map.84 = (bf16[32,2,128,128]{3,2,1,0:T(8,128)(2,1)S(1)}, bf16[128,4096]{1,0:T(8,128)(2,1)S(1)}, bf16[128,4096]{1,0:T(8,128)(2,1)S(1)}, bf16[128,4096]{1,0...) custom-call(bf16[128,4096]{1,0:T(8,128)(2,1)S(1)} %copy-done, ...), custom_call_target="tpu_custom_call" | custom-call | tf_op jit(solution)/shard_map/pallas_call | solution.py:417
  50.1 4.9 %shard_map.85 = (bf16[128,4096]{1,0:T(8,128)(2,1)}, bf16[128,4096]{1,0:T(8,128)(2,1)}, bf16[128,4096]{1,0:T(8,128)(2,1)}, bf16[128,4096]{1,0:T(8,128)(2,1)}) custom-call(bf16[32,2,128,128]{3,2,1,0:T(8,128)(2,1)S(1)} %get-tuple-element.11.states_ref, bf16[128,4096]{1,0:T(8,128)(2,1)S(1)} %get-tuple-element.12.q_ref, ...), custom_call_target="tpu_custom_call" | custom-call | tf_op jit(solution)/shard_map/pallas_call | solution.py:479
Async XLA Ops:
  1.4 1.2 %copy-start = (bf16[128,4096]{1,0:T(8,128)(2,1)S(1)}, bf16[128,4096]{1,0:T(8,128)(2,1)}, u32[]{:S(2)}) copy-start(bf16[128,4096]{1,0:T(8,128)(2,1)} %q_any.1) | copy-start | bytes 3145732
  2.7 1.2 %copy-start.1 = (bf16[128,4096]{1,0:T(8,128)(2,1)S(1)}, bf16[128,4096]{1,0:T(8,128)(2,1)}, u32[]{:S(2)}) copy-start(bf16[128,4096]{1,0:T(8,128)(2,1)} %k_any.1) | copy-start | bytes 3145732
  3.9 1.2 %copy-start.2 = (bf16[128,4096]{1,0:T(8,128)(2,1)S(1)}, bf16[128,4096]{1,0:T(8,128)(2,1)}, u32[]{:S(2)}) copy-start(bf16[128,4096]{1,0:T(8,128)(2,1)} %v_any.1) | copy-start | bytes 3145732
  5.1 1.2 %copy-start.3 = (bf16[128,4096]{1,0:T(8,128)(2,1)S(1)}, bf16[128,4096]{1,0:T(8,128)(2,1)}, u32[]{:S(2)}) copy-start(bf16[128,4096]{1,0:T(8,128)(2,1)} %g_any.1) | copy-start | bytes 3145732

commit v2 on v1

--- a/solution.py
+++ b/solution.py
@@ -19,12 +19,15 @@
     return row >= column
 
 
-def spread_column(decay, head):
+def spread_columns(decay, head, count):
     rows, heads = decay.shape
-    pick = (lax.broadcasted_iota(jnp.int32, (heads, SIZE), 0) == head).astype(F32).astype(BF16)
-    column = jnp.dot(decay, pick, preferred_element_type=F32).astype(BF16)
+    row = lax.broadcasted_iota(jnp.int32, (heads, count * SIZE), 0)
+    column = lax.broadcasted_iota(jnp.int32, (heads, count * SIZE), 1)
+    begin = (row - head) * SIZE
+    pick = ((column >= begin) & (column < begin + SIZE)).astype(F32).astype(BF16)
+    spread = jnp.dot(decay, pick, preferred_element_type=F32).astype(BF16)
     lower = triangle(rows).astype(F32).astype(BF16)
-    return jnp.dot(lower, column, preferred_element_type=F32)
+    return jnp.dot(lower, spread, preferred_element_type=F32)
 
 
 def over_rows(left, right):
@@ -108,6 +111,12 @@
         == lax.broadcasted_iota(jnp.int32, (rows, rows), 1)
     )
     cumul_rows[...] = over_rows(decay, upper.astype(F32).astype(BF16))
+    @pl.loop(0, heads // 4)
+    def _(group):
+        spread = spread_columns(decay, group * 4, 4)
+        for j in range(4):
+            cumuls[group * 4 + j] = spread[:, j * SIZE : (j + 1) * SIZE]
+
     from_planes[z] = jnp.zeros(from_planes.shape[1:], BF16)
     pl.semaphore_wait(barrier, chips + planes - 1)
 
@@ -115,8 +124,7 @@
     fin_copy.start()
 
     def make_terms(head):
-        cumul = spread_column(decay, head)
-        cumuls[head] = cumul
+        cumul = cumuls[head]
         columns = pl.ds(pl.multiple_of(head * SIZE, SIZE), SIZE)
         final = cumul[rows - 1 :, :]
         keys = (k_ref[:, columns].astype(F32) * jnp.exp(final - cumul)).astype(BF16)
@@ -155,17 +163,30 @@
         for copy in loads(owner(step, side), 0):
             copy.wait()
 
-    def first(i, loading=False):
-        @pl.loop(0, chips // 2)
-        def _(pair):
-            steps = (pair * 2, pair * 2 + 1)
+    pairs = chips // 2
+
+    def make(i, pair):
+        steps = (pair * 2, pair * 2 + 1)
+
+        @pl.when(i == 0)
+        def _():
             for step in steps:
-                if loading:
-                    wait_loads(step, 1 - core)
+                wait_loads(step, 1 - core)
+                wait_loads(step, core)
+
+        if own > 1:
+            @pl.when((i == 1) & (pair == 0))
+            def _():
+                @pl.loop(0, devices)
+                def _(group):
+                    for copy in loads(group, 1):
+                        copy.wait()
+
+        for side in (1 - core, core):
             for step in steps:
-                make_terms(owner(step, 1 - core) * own + i)
-            for step in steps:
-                core_copy(i, lax.rem(chip + 1 + step, chips)).start()
+                make_terms(owner(step, side) * own + i)
+        for step in steps:
+            core_copy(i, lax.rem(chip + 1 + step, chips)).start()
 
     def out_copy(i, other):
         return remote(
@@ -179,49 +200,35 @@
             out_r.at[other * own + i], at_chip(other),
         )
 
-    def second(i, loading=False):
-        @pl.loop(0, chips // 2)
-        def _(pair):
-            steps = (pair * 2, pair * 2 + 1)
-            for step in steps:
-                if loading:
-                    wait_loads(step, core)
-            for step in steps:
-                make_terms(owner(step, core) * own + i)
-            for step in steps:
-                core_copy(i, lax.rem(chip + 1 + step, chips)).wait_recv()
-            for step in steps:
-                combine(i, step)
-
     def combine(i, step):
-        if True:
-            other = lax.rem(chip + 1 + step, chips)
-            head = (other * 2 + core) * own + i
-            slot = other * own + i
-            mine = jnp.exp(own_fin[pl.ds(head, 1), :])
-            theirs = jnp.exp(core_fin[pl.ds(head, 1), :])
-            one = jnp.ones_like(mine)
-            kv = (
-                jnp.where(first_core, theirs, one) * terms[head, 0]
-                + jnp.where(first_core, one, mine) * from_core[slot, 0]
-            ).astype(BF16)
-            qd = (
-                jnp.where(first_core, one, theirs) * terms[head, 1]
-                + jnp.where(first_core, mine, one) * from_core[slot, 1]
-            ).astype(BF16)
-
-            @pl.when(step < chips - 1)
-            def _():
-                to_chips[other, i, 0] = kv
-                to_chips[other, i, 1] = qd
-                out_copy(i, other).start()
-
-            @pl.when(step == chips - 1)
-            def _():
-                from_chips[chip, i, 0] = kv
-                from_chips[chip, i, 1] = qd
-
-    first(0, True)
+        other = lax.rem(chip + 1 + step, chips)
+        core_copy(i, other).wait_recv()
+        head = (other * 2 + core) * own + i
+        slot = other * own + i
+        mine = jnp.exp(own_fin[pl.ds(head, 1), :])
+        theirs = jnp.exp(core_fin[pl.ds(head, 1), :])
+        one = jnp.ones_like(mine)
+        kv = (
+            jnp.where(first_core, theirs, one) * terms[head, 0]
+            + jnp.where(first_core, one, mine) * from_core[slot, 0]
+        ).astype(BF16)
+        qd = (
+            jnp.where(first_core, one, theirs) * terms[head, 1]
+            + jnp.where(first_core, mine, one) * from_core[slot, 1]
+        ).astype(BF16)
+
+        @pl.when(step < chips - 1)
+        def _():
+            to_chips[other, i, 0] = kv
+            to_chips[other, i, 1] = qd
+            out_copy(i, other).start()
+
+        @pl.when(step == chips - 1)
+        def _():
+            from_chips[chip, i, 0] = kv
+            from_chips[chip, i, 1] = qd
+
+    make(0, 0)
     fin_copy.wait_recv()
     chip_fin[chip] = own_fin[...] + core_fin[...]
 
@@ -233,17 +240,16 @@
     for step in range(1, chips):
         chip_fin_copy(lax.rem(chip + step, chips), chip).start()
 
-    second(0, True)
-    if own > 1:
-        @pl.loop(0, devices)
-        def _(group):
-            for copy in loads(group, 1):
-                copy.wait()
-
-        @pl.loop(1, own)
-        def _(i):
-            first(i)
-            second(i)
+    def combine_pair(i, pair):
+        for step in (pair * 2, pair * 2 + 1):
+            combine(i, step)
+
+    @pl.loop(1, own * pairs)
+    def _(at):
+        make(at // pairs, lax.rem(at, pairs))
+        combine_pair((at - 1) // pairs, lax.rem(at - 1, pairs))
+
+    combine_pair(own - 1, pairs - 1)
 
     for step in range(1, chips):
         other = lax.rem(chip + step, chips)
@@ -360,7 +366,7 @@
             states_ref[head, 1] = jnp.where(first_core, early, trail).astype(BF16)
 
     events = []
-    lead = min(3, own)
+    lead = min(2, own)
     for i in range(lead):
         events.append((sum_plane, i))
     for i in range(own):
@@ -409,6 +415,7 @@
 
 def carried_states(planes, devices, arrays):
     decay = arrays[-1]
+    arrays = [pltpu.with_memory_space_constraint(item, pltpu.HBM) for item in arrays[:-1]] + [decay]
     heads = decay.shape[1]
     chips, own = devices // 2, heads // devices
     square = (SIZE, SIZE)

time: 55.3 us -> 43.1 us (0.78)
  Pallas kernels: 48.6 us -> 41.4 us
  local copies, waits for them, and re-layouts: 5.71 us -> 0.81 us
    pallas_call x1, Pallas kernels: 43.7 us -> 36.6 us  [carried_states(): pl.pallas_call(functools.partial(states_kernel, planes, devices), out_sha...]
    unnamed x9 -> x1, local copies, waits for them, and re-layouts: 5.71 us -> 0.81 us
where the time goes in v2:
time: 43.1 us; the launch traced here: 42.9 us
  Pallas kernels  41.4 us (96%)
  local copies, waits for them, and re-layouts  0.81 us (2%)
  between operations  0.64 us (1%)
    pallas_call x1, Pallas kernels, carried_states(): pl.pallas_call(functools.partial(states_kernel, planes, devices), out_sha...  36.6 us
    pallas_call x1, Pallas kernels, block_results(): pl.pallas_call(functools.partial(block_kernel, group), grid=(features //...  4.89 us

profile of v2, /device:TPU:0, one launch (start us, length us, event | category | flops | bytes accessed | tf_op | source)
XLA Modules:
  0.0 42.9 jit_solution(11946700042612433656)
XLA Ops:
  0.6 0.8 %copy.9.decay_ref = bf16[128,32]{1,0:T(8,128)(2,1)S(1)} copy(bf16[128,32]{0,1:T(8,128)(2,1)} %param.9) | data formatting | bytes 16384 | tf_op args[4]
  1.4 36.6 %shard_map.84 = (bf16[32,2,128,128]{3,2,1,0:T(8,128)(2,1)S(1)}, bf16[128,4096]{1,0:T(8,128)(2,1)S(1)}, bf16[128,4096]{1,0:T(8,128)(2,1)S(1)}, bf16[128,4096]{1,0...) custom-call(bf16[128,4096]{1,0:T(8,128)(2,1)} %q_any.1, ...), custom_call_target="tpu_custom_call" | custom-call | tf_op jit(solution)/shard_map/pallas_call | solution.py:424
  38.0 4.9 %shard_map.85 = (bf16[128,4096]{1,0:T(8,128)(2,1)}, bf16[128,4096]{1,0:T(8,128)(2,1)}, bf16[128,4096]{1,0:T(8,128)(2,1)}, bf16[128,4096]{1,0:T(8,128)(2,1)}) custom-call(bf16[32,2,128,128]{3,2,1,0:T(8,128)(2,1)S(1)} %get-tuple-element.11.states_ref, bf16[128,4096]{1,0:T(8,128)(2,1)S(1)} %get-tuple-element.12.q_ref, ...), custom_call_target="tpu_custom_call" | custom-call | tf_op jit(solution)/shard_map/pallas_call | solution.py:486

commit v3 on v2

--- a/solution.py
+++ b/solution.py
@@ -482,7 +482,7 @@
 
 def block_results(held):
     rows, features = held[1].shape
-    group = 4
+    group = 8
     return pl.pallas_call(
         functools.partial(block_kernel, group),
         grid=(features // (group * SIZE),),

time: 43.1 us -> 42 us (0.974)
  Pallas kernels: 41.4 us -> 40.3 us
    pallas_call x1, Pallas kernels: 4.89 us -> 3.76 us  [block_results(): pl.pallas_call(functools.partial(block_kernel, group), grid=(features //...]
where the time goes in v3:
time: 42 us; the launch traced here: 41.8 us
  Pallas kernels  40.3 us (96%)
  local copies, waits for them, and re-layouts  0.81 us (2%)
  between operations  0.64 us (2%)
    pallas_call x1, Pallas kernels, carried_states(): pl.pallas_call(functools.partial(states_kernel, planes, devices), out_sha...  36.6 us
    pallas_call x1, Pallas kernels, block_results(): pl.pallas_call(functools.partial(block_kernel, group), grid=(features //...  3.76 us

profile of v3, /device:TPU:0, one launch (start us, length us, event | category | flops | bytes accessed | tf_op | source)
XLA Modules:
  0.0 41.8 jit_solution(3085019303697599624)
XLA Ops:
  0.6 0.8 %copy.9.decay_ref = bf16[128,32]{1,0:T(8,128)(2,1)S(1)} copy(bf16[128,32]{0,1:T(8,128)(2,1)} %param.9) | data formatting | bytes 16384 | tf_op args[4]
  1.4 36.6 %shard_map.84 = (bf16[32,2,128,128]{3,2,1,0:T(8,128)(2,1)S(1)}, bf16[128,4096]{1,0:T(8,128)(2,1)S(1)}, bf16[128,4096]{1,0:T(8,128)(2,1)S(1)}, bf16[128,4096]{1,0...) custom-call(bf16[128,4096]{1,0:T(8,128)(2,1)} %q_any.1, ...), custom_call_target="tpu_custom_call" | custom-call | tf_op jit(solution)/shard_map/pallas_call | solution.py:424
  38.0 3.8 %shard_map.85 = (bf16[128,4096]{1,0:T(8,128)(2,1)}, bf16[128,4096]{1,0:T(8,128)(2,1)}, bf16[128,4096]{1,0:T(8,128)(2,1)}, bf16[128,4096]{1,0:T(8,128)(2,1)}) custom-call(bf16[32,2,128,128]{3,2,1,0:T(8,128)(2,1)S(1)} %get-tuple-element.11.states_ref, bf16[128,4096]{1,0:T(8,128)(2,1)S(1)} %get-tuple-element.12.q_ref, ...), custom_call_target="tpu_custom_call" | custom-call | tf_op jit(solution)/shard_map/pallas_call | solution.py:486
